TPU v7x, 32 devices: a whole 2x2x4 slice. The times are simulated.
32 devices in a mesh: groups: 2 (over y), seq: 4 (over z), tensor: 2 (over x), cfg: 2 (over core).
Axes of the slice: x: 2, y: 2, z: 4, core: 2. Of those that a mesh axis runs over, the one named last changes fastest.
Arguments:
- latent: bfloat16 [2048, 3072], P(('groups', 'seq')), parts along dimension 0, may hold values from -6 to 6
- positions: int32 [3, 2048], P(None, ('groups', 'seq')), parts along dimension 1, may hold values from 0 to 79, as said below
- text_kv: bfloat16 [2, 2, 128, 3072], P('cfg', None, ('groups', 'seq'), 'tensor'), parts along dimension 2, may hold values from -6 to 6
- text_len: int32 [4], P(('groups', 'cfg')), parts along dimension 0, may hold values from 1 to 64
- modulation: float32 [3, 4, 3072], P(None, 'groups'), parts along dimension 1, may hold values from -3 to 3
- w_qkv: bfloat16 [3, 3072, 3072], P(None, 'cfg', 'tensor'), may hold values from -0.109375 to 0.109375
- norm_gains: float32 [2, 128], replicated, may hold values from 0.5 to 2.5
- w_out: bfloat16 [3072, 3072], P('tensor', 'cfg'), may hold values from -0.109375 to 0.109375
- guidance: float32 [2], P('groups'), parts along dimension 0, may hold values from 3 to 8
Outputs:
- guided: bfloat16 [2048, 3072], P(('groups', 'seq', 'tensor'), 'cfg'), parts along dimension 0
There are 2 independent parts, one for each index of `groups`. A program takes and returns all parts, laid end to end along the dimension named above; an argument that names none is the same for every part. Nothing has to cross between parts.
Inputs may be any that keep to these rules, and one draw needn't show every extreme that they name: `positions`: frame indices are below 33, height indices below 45, width indices below 80. `text_len`: text rows at or beyond the count are ignored.
All inputs are finite; a program needn't handle non-finite values.
Results may differ from a plain program's by a relative error of at most 0.018.
Values may be sent and summed in bfloat16 or wider, within the bound.
A program may use at most 128 MiB of HBM per device.

v0:
```python
import jax
import jax.numpy as jnp
from jax import lax
from jax.sharding import PartitionSpec as P

HEAD_DIM = 128


def swapped(value, axis, apart):
    mask = 2**apart
    pairs = [(source, source ^ mask) for source in range(lax.axis_size(axis))]
    return lax.ppermute(value, axis, pairs)


def head_norm(heads_in, gain):
    return (
        heads_in * lax.rsqrt(jnp.mean(heads_in * heads_in, axis=-1, keepdims=True) + 1e-06) * gain
    )


def rotary(heads_in, positions):
    head_size = heads_in.shape[-1]
    blocks = (head_size // 8, 7 * head_size // 16, 7 * head_size // 16)
    pieces = []
    offset = 0
    for axis_id in range(3):
        width = blocks[axis_id]
        half = width // 2
        freq = 256.0 ** (-jnp.arange(half, dtype=jnp.float32) / half)
        angle = positions[axis_id].astype(jnp.float32)[:, None] * freq[None, :]
        cosine = jnp.cos(angle)[:, None, :]
        sine = jnp.sin(angle)[:, None, :]
        first = heads_in[..., offset : offset + half]
        second = heads_in[..., offset + half : offset + width]
        pieces.append(first * cosine - second * sine)
        pieces.append(second * cosine + first * sine)
        offset = offset + width
    return jnp.concatenate(pieces, axis=-1)


def local(latent, positions, text_kv, text_len, modulation, w_qkv, norm_gains, w_out, guidance):
    rows_here = latent.shape[0]
    width_dev = w_qkv.shape[2]
    heads_dev = width_dev // HEAD_DIM
    text_dev = text_kv.shape[2]
    branch = lax.axis_index("cfg")
    xfloat = latent.astype(jnp.float32)
    center = xfloat - jnp.mean(xfloat, axis=-1, keepdims=True)
    normed = center * lax.rsqrt(jnp.mean(center * center, axis=-1, keepdims=True) + 1e-06)
    both_mod = (
        normed[None] * (1.0 + modulation[1][:, None, :]) + modulation[0][:, None, :]
    ).astype(jnp.bfloat16)
    rows_w = w_qkv.shape[1]
    columns = lax.dynamic_slice_in_dim(both_mod, branch * rows_w, rows_w, 2)
    terms = jnp.einsum("btd,jde->bjte", columns, w_qkv, preferred_element_type=jnp.float32)
    projected = lax.psum_scatter(
        terms.astype(jnp.bfloat16), "cfg", scatter_dimension=0, tiled=True
    ).astype(jnp.float32)[0]
    queries = rotary(
        head_norm(projected[0].reshape(rows_here, heads_dev, HEAD_DIM), norm_gains[0]), positions
    ).astype(jnp.bfloat16)
    keys = rotary(
        head_norm(projected[1].reshape(rows_here, heads_dev, HEAD_DIM), norm_gains[1]), positions
    ).astype(jnp.bfloat16)
    keys = keys.reshape(rows_here, width_dev)
    value_rows = projected[2].astype(jnp.bfloat16)
    text_raw = text_kv[0, 0].astype(jnp.float32).reshape(text_dev, heads_dev, HEAD_DIM)
    text_keys = head_norm(text_raw, norm_gains[1]).astype(jnp.bfloat16).reshape(text_dev, width_dev)
    text_values = text_kv[0, 1]
    length = text_len[0]
    scale = HEAD_DIM ** (-0.5)

    def attend(carry, key_rows, val_rows, valid):
        running_sum, accum = carry
        count = key_rows.shape[0]
        key_heads = key_rows.reshape(count, heads_dev, HEAD_DIM)
        val_heads = val_rows.reshape(count, heads_dev, HEAD_DIM)
        scores = (
            jnp.einsum("thd,nhd->htn", queries, key_heads, preferred_element_type=jnp.float32)
            * scale
        )
        expo = jnp.where(valid[None, None, :], jnp.exp(scores), 0.0)
        new_sum = running_sum + jnp.sum(expo, axis=-1)
        new_acc = accum + jnp.einsum(
            "htn,nhd->htd", expo.astype(jnp.bfloat16), val_heads, preferred_element_type=jnp.float32
        )
        return (new_sum, new_acc)

    start_state = (
        jnp.zeros((heads_dev, rows_here), jnp.float32),
        jnp.zeros((heads_dev, rows_here, HEAD_DIM), jnp.float32),
    )
    carry = start_state
    image_keys = lax.all_gather(keys, "seq", axis=0, tiled=True)
    image_values = lax.all_gather(value_rows, "seq", axis=0, tiled=True)
    prompt_keys = lax.all_gather(text_keys, "seq", axis=0, tiled=True)
    prompt_values = lax.all_gather(text_values, "seq", axis=0, tiled=True)
    carry = attend(carry, image_keys, image_values, jnp.ones((image_keys.shape[0],), bool))
    text_index = jnp.arange(prompt_keys.shape[0], dtype=jnp.int32)
    state = attend(carry, prompt_keys, prompt_values, text_index < length)
    final_sum, final_acc = state
    attended = (
        (final_acc / final_sum[..., None])
        .transpose(1, 0, 2)
        .reshape(rows_here, width_dev)
        .astype(jnp.bfloat16)
    )
    strength = guidance[0]
    half_cols = w_out.shape[1]
    full_out = lax.all_gather(w_out, "cfg", axis=1, tiled=True)
    summed = lax.psum_scatter(
        jnp.dot(attended, full_out, preferred_element_type=jnp.float32).astype(jnp.bfloat16),
        "tensor",
        scatter_dimension=0,
        tiled=True,
    ).astype(jnp.float32)
    gate = lax.dynamic_index_in_dim(modulation[2], branch, 0, keepdims=False)
    mine = (gate * summed).astype(jnp.bfloat16)
    own_half = lax.dynamic_slice_in_dim(mine, branch * half_cols, half_cols, 1)
    send_half = lax.dynamic_slice_in_dim(mine, (1 - branch) * half_cols, half_cols, 1)
    other = swapped(send_half, "cfg", 0)
    cond_rows = jnp.where(branch == 0, own_half, other).astype(jnp.float32)
    uncond_rows = jnp.where(branch == 0, other, own_half).astype(jnp.float32)
    guided = (uncond_rows + strength * (cond_rows - uncond_rows)).astype(jnp.bfloat16)
    return guided


def solution(mesh):
    placed = (
        P(("groups", "seq"), None),
        P(None, ("groups", "seq")),
        P("cfg", None, ("groups", "seq"), "tensor"),
        P(("groups", "cfg")),
        P(None, "groups", None),
        P(None, "cfg", "tensor"),
        P(),
        P("tensor", "cfg"),
        P("groups"),
    )
    return jax.shard_map(
        local,
        mesh=mesh,
        in_specs=placed,
        out_specs=P(("groups", "seq", "tensor"), "cfg"),
        check_vma=False,
    )
```

profile of v0, /device:TPU:0, one launch (start us, length us, event | category | flops | bytes accessed | tf_op | source)
XLA Modules:
  0.0 247.0 jit_solution(18201941797049536414)
XLA Ops:
  6.5 1.5 fusion.31
  8.1 1.7 convert_reduce_fusion
  9.8 0.6 fusion.11
  10.3 2.3 fusion.9
  12.6 1.5 constant_dynamic-slice_fusion.1
  14.1 14.2 %convert_bitcast_fusion = bf16[2,3,256,1536]{3,2,1,0:T(8,128)(2,1)} fusion(bf16[3,1536,1536]{2,1,0:T(8,128)(2,1)} %param.14, f32[2,1536]{1,0:T(2,128)S(1)} %get-tuple-element.46, f32[2,1536]{1,0:T(2,128)S(1)} %get-tuple-element.45, f32[256,1536]{1,0:T(8,128)S(1)} %constant_dynamic-slice_fusion.1), kind=kOutput, calls=%fused_computation.7 | convolution fusion | flops 7252475904 | bytes 20471808 | tf_op jit(solution)/shard_map/btd,jde->bjte/dot_general | solution.py:55
  28.4 15.3 %reduce-scatter.3.cloned.1.call-done = bf16[1,3,256,1536]{3,2,1,0:T(8,128)(2,1)} async-done(((bf16[2,3,256,1536]{3,2,1,0:T(8,128)(2,1)}), bf16[1,3,256,1536]{3,2,1,0:T(8,128)(2,1)}) %reduce-scatter.3.cloned.1.call-update) | async-done | bytes 2359312 | tf_op jit(solution)/shard_map/reduce_scatter | solution.py:56
  43.7 2.3 slice.122
  46.2 0.8 copy.24
  47.0 0.8 copy.25
  47.8 1.5 multiply_cosine_fusion
  49.4 2.0 fusion.30
  51.4 1.9 copy.22
  53.3 1.6 copy.23
  54.9 2.0 copy.26
  56.9 1.6 copy.27
  58.8 1.1 copy-done.2
  60.0 0.5 multiply_multiply_fusion.1
  60.4 0.9 copy-done.3
  61.4 0.5 multiply_multiply_fusion
  62.3 3.3 %add_convert_fusion.1 = (bf16[256,12,28]{2,0,1:T(8,128)(2,1)}, bf16[256,12,28]{2,0,1:T(8,128)(2,1)}, bf16[256,12,28]{2,0,1:T(8,128)(2,1)}, bf16[256,12,28]{2,0,1:T(8,128)(2,1)}) fusion(f32[256,12,128]{2,0,1:T(8,128)S(1)} %multiply_multiply_fusion, f32[256,28]{1,0:T(8,128)S(1)} %get-tuple-element.32, f32[256,28]{1,0:T(8,128)S(1)} %get-tuple-element.31, ...), kind=kLoop, calls=%fused_computation.22 | loop fusion | flops 1376256 | bytes 2179072 | tf_op jit(solution)/shard_map/convert.7
  65.6 2.3 add_convert_fusion.3
  67.9 5.8 %concatenate.9 = bf16[256,12,128]{2,0,1:T(8,128)(2,1)} concatenate(bf16[256,12,8]{2,0,1:T(8,128)(2,1)} %get-tuple-element.12, bf16[256,12,8]{2,0,1:T(8,128)(2,1)} %get-tuple-element.11, bf16[256,12,28]{2,0,1:T(8,128)(2,1)} %get-tuple-element.19, bf16[256,12,28]{2,0,1:T(8,128)(2,1)} %get-tuple-element.20, bf16[256,12,28]{2,0,1:T(8,128)(2,1)} %get-tuple-element.8, ...), dimensions={2} | concatenate | bytes 1572864 | tf_op jit(solution)/shard_map/concatenate | solution.py:38
  73.7 2.3 copy.28
  76.1 0.5 all-gather.8.cloned.1.call-update
  76.7 1.4 slice.107
  78.1 1.4 convert_multiply_fusion
  79.5 1.6 mul.442
  81.8 17.6 %all-gather.1 = bf16[1,1,64,1536]{3,2,1,0:T(8,128)(2,1)} all-gather(bf16[1,1,16,1536]{3,2,1,0:T(8,128)(2,1)} %slice.107), channel_id=3, replica_groups=mesh['groups'=2,'seq'=4,'tensor'=2,'cfg'=2] {'seq'}, dimensions={2}, use_global_device_ids=true | all-gather | bytes 245760 | tf_op jit(solution)/shard_map/all_gather | solution.py:97
  99.4 1.8 reshape.268
  101.2 1.0 reduce_sum.67
  102.3 0.8 fusion.28
  103.1 15.8 %all_gather.17 = bf16[64,1536]{1,0:T(8,128)(2,1)} all-gather(bf16[16,1536]{1,0:T(8,128)(2,1)S(1)} %fusion.28), channel_id=1, replica_groups=mesh['groups'=2,'seq'=4,'tensor'=2,'cfg'=2] {'seq'}, dimensions={0}, use_global_device_ids=true | all-gather | bytes 245760 | tf_op jit(solution)/shard_map/all_gather | solution.py:96
  118.9 4.2 %add_convert_fusion.4 = (bf16[256,12,28]{2,0,1:T(8,128)(2,1)}, bf16[256,12,28]{2,0,1:T(8,128)(2,1)}, bf16[256,12,28]{2,0,1:T(8,128)(2,1)}, bf16[256,12,28]{2,0,1:T(8,128)(2,1)}) fusion(f32[256,12,128]{2,0,1:T(8,128)S(1)} %multiply_multiply_fusion.1, f32[256,28]{1,0:T(8,128)S(1)} %get-tuple-element.32, f32[256,28]{1,0:T(8,128)S(1)} %get-tuple-element.31, ...), kind=kLoop, calls=%fused_computation.30 | loop fusion | flops 1376256 | bytes 2179072 | tf_op jit(solution)/shard_map/convert.13
  123.2 4.6 %concatenate.8 = bf16[256,12,128]{2,0,1:T(8,128)(2,1)S(1)} concatenate(bf16[256,12,8]{2,0,1:T(8,128)(2,1)S(1)} %get-tuple-element.23, bf16[256,12,8]{2,0,1:T(8,128)(2,1)S(1)} %get-tuple-element.24, bf16[256,12,28]{2,0,1:T(8,128)(2,1)} %get-tuple-element.21, bf16[256,12,28]{2,0,1:T(8,128)(2,1)} %get-tuple-element.22, bf16[256,12,28]{2,0,1:T(8,128)(2,1)} %get-tuple-element.14, ...), dimensions={2} | concatenate | bytes 1572864 | tf_op jit(solution)/shard_map/concatenate | solution.py:38
  127.8 1.2 fusion.32
  129.0 4.7 %copy.30 = bf16[1,1,1024,1536]{2,3,1,0:T(8,128)(2,1)} copy(bf16[1,1,1024,1536]{3,2,1,0:T(8,128)(2,1)} %all-gather.10.cloned.1.call-done) | data formatting | bytes 6291456 | tf_op jit(solution)/shard_map/all_gather | solution.py:95
  133.7 46.5 %all-gather.6.cloned.1.call-done = bf16[1024,1536]{0,1:T(8,128)(2,1)} async-done(((bf16[256,1536]{0,1:T(8,128)(2,1)}), bf16[1024,1536]{0,1:T(8,128)(2,1)}) %all-gather.6.cloned.1.call-update) | async-done | bytes 3145744 | tf_op jit(solution)/shard_map/all_gather | solution.py:94
  180.2 4.1 %fusion.2 = (f32[12,256]{1,0:T(8,128)S(1)}, f32[12,256,1024]{2,1,0:T(8,128)S(1)}) fusion(bf16[256,12,128]{2,0,1:T(8,128)(2,1)} %copy-done.4, bf16[1024,12,128]{0,2,1:T(8,128)(2,1)} %bitcast.78), kind=kOutput, calls=%fused_computation.3 | convolution fusion | flops 811594752 | bytes 16527360 | tf_op jit(solution)/shard_map/thd,nhd->htn/dot_general | solution.py:79
  184.4 5.6 %fusion.4 = f32[12,256,128]{1,2,0:T(8,128)} fusion(bf16[1024,12,128]{0,2,1:T(8,128)(2,1)} %bitcast.77, f32[12,256,1024]{2,1,0:T(8,128)S(1)} %get-tuple-element.42), kind=kOutput, calls=%fused_computation.5 | convolution fusion | flops 811597824 | bytes 17301504 | tf_op jit(solution)/shard_map/htn,nhd->htd/dot_general | solution.py:84
  190.0 2.4 fusion.17
  192.4 9.1 %all-gather.8.cloned.1.call-done = bf16[1536,3072]{1,0:T(8,128)(2,1)} async-done(((bf16[1536,1536]{1,0:T(8,128)(2,1)}), bf16[1536,3072]{1,0:T(8,128)(2,1)}) %all-gather.8.cloned.1.call-update) | async-done | bytes 9437200 | tf_op jit(solution)/shard_map/all_gather | solution.py:110
  201.5 7.4 %convolution_convert_fusion = bf16[256,3072]{1,0:T(8,128)(2,1)} fusion(bf16[256,1536]{0,1:T(8,128)(2,1)S(1)} %bitcast.80, bf16[1536,3072]{1,0:T(8,128)(2,1)} %all-gather.8.cloned.1.call-done), kind=kOutput, calls=%fused_computation.10 | convolution fusion | flops 2416705536 | bytes 11796480 | tf_op jit(solution)/shard_map/dot_general | solution.py:112
  208.9 0.7 copy-done.10
  209.7 26.7 %reduce-scatter.5.cloned.1.call-done = bf16[128,3072]{1,0:T(8,128)(2,1)} async-done(((bf16[256,3072]{1,0:T(8,128)(2,1)}), bf16[128,3072]{1,0:T(8,128)(2,1)}) %reduce-scatter.5.cloned.1.call-update) | async-done | bytes 786448 | tf_op jit(solution)/shard_map/reduce_scatter | solution.py:111
  236.4 1.3 multiply_convert_fusion
  238.5 1.1 collective-permute-done
  239.5 0.9 fusion.21
  (53 shorter events, 1.4 us)
Async XLA Ops:
  6.5 3.2 %copy-start = (bf16[256,3072]{1,0:T(8,128)(2,1)S(1)}, bf16[256,3072]{1,0:T(8,128)(2,1)}, u32[]{:S(2)}) copy-start(bf16[256,3072]{1,0:T(8,128)(2,1)} %param.9) | copy-start | bytes 4718596
  6.5 37.2 %reduce-scatter.3.cloned.1.call-start = ((), (), s32[]{:S(2)}) async-start(), calls=%async_computation.2 | async-start | bytes 7077888 | tf_op jit(solution)/shard_map/reduce_scatter | solution.py:56
  28.3 17.8 %copy-start.11 = (s32[3,256]{1,0:T(4,128)S(1)}, s32[3,256]{1,0:T(4,128)}, u32[]{:S(2)}) copy-start(s32[3,256]{1,0:T(4,128)} %param.10) | copy-start | bytes 9220
  28.3 19.5 %copy-start.12 = (f32[2,128]{1,0:T(2,128)S(1)}, f32[2,128]{1,0:T(2,128)}, u32[]{:S(2)}) copy-start(f32[2,128]{1,0:T(2,128)} %param.15) | copy-start | bytes 3076
  28.3 100.7 %all-gather.10.cloned.1.call-start = ((), (), s32[]{:S(2)}) async-start(), calls=%async_computation.6 | async-start | bytes 3932160 | tf_op jit(solution)/shard_map/all_gather | solution.py:95
  43.7 5.7 %copy-start.1 = (bf16[1,3,256,1536]{3,2,1,0:T(8,128)(2,1)S(1)}, bf16[1,3,256,1536]{3,2,1,0:T(8,128)(2,1)}, u32[]{:S(2)}) copy-start(bf16[1,3,256,1536]{3,2,1,0:T(8,128)(2,1)} %reduce-scatter.3.cloned.1.call-done) | copy-start | bytes 7077892
  46.0 134.2 %all-gather.6.cloned.1.call-start = ((), (), s32[]{:S(2)}) async-start(), calls=%async_computation.3 | async-start | bytes 3932160 | tf_op jit(solution)/shard_map/all_gather | solution.py:94
  58.5 1.4 copy-start.2
  60.0 1.4 copy-start.3
  61.4 0.9 copy-start.5
  62.3 3.3 %copy-start.6 = (f32[256,8]{1,0:T(8,128)S(1)}, f32[256,8]{1,0:T(8,128)}, u32[]{:S(2)}) copy-start(f32[256,8]{1,0:T(8,128)} %copy.24) | copy-start | bytes 24580
  62.3 3.3 %copy-start.7 = (f32[256,8]{1,0:T(8,128)S(1)}, f32[256,8]{1,0:T(8,128)}, u32[]{:S(2)}) copy-start(f32[256,8]{1,0:T(8,128)} %copy.25) | copy-start | bytes 24580
  76.0 125.4 %all-gather.8.cloned.1.call-start = ((), (), s32[]{:S(2)}) async-start(), calls=%async_computation.4 | async-start | bytes 14155776 | tf_op jit(solution)/shard_map/all_gather | solution.py:110
  76.6 159.8 %reduce-scatter.5.cloned.1.call-start = ((), (), s32[]{:S(2)}) async-start(), calls=%async_computation.5 | async-start | bytes 2359296 | tf_op jit(solution)/shard_map/reduce_scatter | solution.py:111
  123.2 4.6 %copy-start.9 = (bf16[64,1536]{1,0:T(8,128)(2,1)S(1)}, bf16[64,1536]{1,0:T(8,128)(2,1)}, u32[]{:S(2)}) copy-start(bf16[64,1536]{1,0:T(8,128)(2,1)} %all_gather.17) | copy-start | bytes 589828
  127.8 5.9 %copy-start.4 = (bf16[256,12,128]{2,0,1:T(8,128)(2,1)}, bf16[256,12,128]{2,0,1:T(8,128)(2,1)S(1)}, u32[]{:S(2)}) copy-start(bf16[256,12,128]{2,0,1:T(8,128)(2,1)S(1)} %concatenate.8) | copy-start | bytes 2359300
  184.4 5.6 %copy-start.8 = (bf16[64,12,128]{2,1,0:T(8,128)(2,1)S(1)}, bf16[64,12,128]{2,1,0:T(8,128)(2,1)}, u32[]{:S(2)}) copy-start(bf16[64,12,128]{2,1,0:T(8,128)(2,1)} %reshape.268) | copy-start | bytes 589828
  208.9 0.7 copy-start.10
  237.7 1.8 collective-permute-start
Sparse Core Ops, SparseCore 0:
  28.4 15.2 reduce-scatter.2
  46.1 70.3 all-gather.9
  118.1 62.0 all-gather.5
  181.6 19.7 all-gather.7
  209.0 27.3 reduce-scatter.4
where the time goes:
time: 248 us; the launch traced here: 247 us
  waiting for transfers between devices  99.3 us (40%)
  local copies, waits for them, and re-layouts  40.1 us (16%)
  matrix products  34.9 us (14%)
  blocking collectives  33.4 us (13%)
  other arithmetic  24.3 us (10%)
  between operations  14.7 us (6%)
    all_gather x1, waiting for transfers between devices, local(): image_keys = lax.all_gather(keys, 'seq', axis=0, tiled=True)  46.5 us
    reduce_scatter x1, waiting for transfers between devices, local(): lax.psum_scatter(jnp.dot(attended, full_out, preferred_element_type=jnp.f...  26.7 us
    all_gather x1, blocking collectives, local(): prompt_values = lax.all_gather(text_values, 'seq', axis=0, tiled=True)  17.6 us
    all_gather x1, blocking collectives, local(): prompt_keys = lax.all_gather(text_keys, 'seq', axis=0, tiled=True)  15.8 us
    reduce_scatter x1, waiting for transfers between devices, local(): lax.psum_scatter(terms.astype(jnp.bfloat16), 'cfg', scatter_dimension=0,...  15.3 us
    dot_general x1, matrix products, local(): jnp.einsum('btd,jde->bjte', columns, w_qkv, preferred_element_type=jnp.fl...  14.2 us
    concatenate x3, local copies, waits for them, and re-layouts, rotary(): return jnp.concatenate(pieces, axis=-1)  12.8 us
    another operation x3, other arithmetic  9.86 us
  transfers between devices with their start and end apart: 6, of which 5 were waited for; matrix products, arithmetic and copies ran while one was open for 25% of the time, Pallas kernels for 0%

commit v1 on v0

--- a/solution.py
+++ b/solution.py
@@ -39,6 +39,13 @@
 
 
 def local(latent, positions, text_kv, text_len, modulation, w_qkv, norm_gains, w_out, guidance):
+
+    def mix_samples_all_here(q_in, unit, net_axis):
+        finding = lax.all_gather(
+            jnp.concatenate([q_in, unit], axis=1), net_axis, axis=0, tiled=True
+        )
+        return jnp.split(finding, [q_in.shape[1]], axis=1)
+
     rows_here = latent.shape[0]
     width_dev = w_qkv.shape[2]
     heads_dev = width_dev // HEAD_DIM
@@ -91,8 +98,7 @@
         jnp.zeros((heads_dev, rows_here, HEAD_DIM), jnp.float32),
     )
     carry = start_state
-    image_keys = lax.all_gather(keys, "seq", axis=0, tiled=True)
-    image_values = lax.all_gather(value_rows, "seq", axis=0, tiled=True)
+    image_keys, image_values = mix_samples_all_here(keys, value_rows, "seq")
     prompt_keys = lax.all_gather(text_keys, "seq", axis=0, tiled=True)
     prompt_values = lax.all_gather(text_values, "seq", axis=0, tiled=True)
     carry = attend(carry, image_keys, image_values, jnp.ones((image_keys.shape[0],), bool))

time: 248 us -> 259 us (1.044)
  waiting for transfers between devices: 99.3 us -> 109 us
  blocking collectives: 33.4 us -> 36 us
    all_gather x2 -> x1, waiting for transfers between devices: 46.5 us -> 71.4 us  [mix_samples_all_here(): lax.all_gather(jnp.concatenate([q_in, unit], axis=1), net_axis, axis=0, t...]
    split x0 -> x3, local copies, waits for them, and re-layouts: none -> 12.8 us  [mix_samples_all_here(): return jnp.split(finding, [q_in.shape[1]], axis=1)]
    all_gather x1, waiting for transfers between devices: 9.06 us -> 0.02 us  [local(): full_out = lax.all_gather(w_out, 'cfg', axis=1, tiled=True)]
    all_gather x1, blocking collectives: 15.8 us -> 21 us  [local(): prompt_keys = lax.all_gather(text_keys, 'seq', axis=0, tiled=True)]
    all_gather x1 -> x0, local copies, waits for them, and re-layouts: 4.69 us -> none  [local(): image_values = lax.all_gather(value_rows, 'seq', axis=0, tiled=True)]
    reduce_scatter x1, waiting for transfers between devices: 15.3 us -> 11 us  [local(): lax.psum_scatter(terms.astype(jnp.bfloat16), 'cfg', scatter_dimension=0,...]
    all_gather x1, blocking collectives: 17.6 us -> 15 us  [local(): prompt_values = lax.all_gather(text_values, 'seq', axis=0, tiled=True)]
  transfers between devices with their start and end apart: 6 -> 5, of which waited for: 5 -> 4; matrix products, arithmetic and copies ran while one was open for 25% -> 15% of each run, Pallas kernels for 0% -> 0%
where the time goes in v1:
time: 259 us; the launch traced here: 258 us
  waiting for transfers between devices  109 us (42%)
  local copies, waits for them, and re-layouts  41 us (16%)
  blocking collectives  36 us (14%)
  matrix products  34.3 us (13%)
  other arithmetic  22.6 us (9%)
  between operations  14.8 us (6%)
    all_gather x1, waiting for transfers between devices, mix_samples_all_here(): lax.all_gather(jnp.concatenate([q_in, unit], axis=1), net_axis, axis=0, t...  71.4 us
    reduce_scatter x1, waiting for transfers between devices, local(): lax.psum_scatter(jnp.dot(attended, full_out, preferred_element_type=jnp.f...  25 us
    all_gather x1, blocking collectives, local(): prompt_keys = lax.all_gather(text_keys, 'seq', axis=0, tiled=True)  21 us
    all_gather x1, blocking collectives, local(): prompt_values = lax.all_gather(text_values, 'seq', axis=0, tiled=True)  15 us
    dot_general x1, matrix products, local(): jnp.einsum('btd,jde->bjte', columns, w_qkv, preferred_element_type=jnp.fl...  14.1 us
    split x3, local copies, waits for them, and re-layouts, mix_samples_all_here(): return jnp.split(finding, [q_in.shape[1]], axis=1)  12.8 us
    concatenate x3, local copies, waits for them, and re-layouts, rotary(): return jnp.concatenate(pieces, axis=-1)  11.4 us
    reduce_scatter x1, waiting for transfers between devices, local(): lax.psum_scatter(terms.astype(jnp.bfloat16), 'cfg', scatter_dimension=0,...  11 us
  transfers between devices with their start and end apart: 5, of which 4 were waited for; matrix products, arithmetic and copies ran while one was open for 15% of the time, Pallas kernels for 0%

profile of v1, /device:TPU:0, one launch (start us, length us, event | category | flops | bytes accessed | tf_op | source)
XLA Modules:
  0.0 258.1 jit_solution(16085171058808939353)
XLA Ops:
  6.5 1.5 fusion.32
  8.0 1.7 convert_reduce_fusion
  9.8 0.6 fusion.11
  10.3 2.3 fusion.9
  12.6 1.5 constant_dynamic-slice_fusion.1
  14.1 14.1 %convert_bitcast_fusion = bf16[2,3,256,1536]{3,2,1,0:T(8,128)(2,1)} fusion(bf16[3,1536,1536]{2,1,0:T(8,128)(2,1)} %param.14, f32[2,1536]{1,0:T(2,128)S(1)} %get-tuple-element.48, f32[2,1536]{1,0:T(2,128)S(1)} %get-tuple-element.47, f32[256,1536]{1,0:T(8,128)S(1)} %constant_dynamic-slice_fusion.1), kind=kOutput, calls=%fused_computation.7 | convolution fusion | flops 7252475904 | bytes 20471808 | tf_op jit(solution)/shard_map/btd,jde->bjte/dot_general | solution.py:62
  28.4 0.6 copy-done.13
  29.1 0.8 copy.29
  29.9 0.8 copy.28
  30.7 0.6 slice_bitcast_fusion.3
  31.3 1.5 multiply_cosine_fusion
  32.8 11.0 %reduce-scatter.3.cloned.1.call-done = bf16[1,3,256,1536]{3,2,1,0:T(8,128)(2,1)} async-done(((bf16[2,3,256,1536]{3,2,1,0:T(8,128)(2,1)}), bf16[1,3,256,1536]{3,2,1,0:T(8,128)(2,1)}) %reduce-scatter.3.cloned.1.call-update) | async-done | bytes 2359312 | tf_op jit(solution)/shard_map/reduce_scatter | solution.py:63
  43.7 2.9 %fusion.31 = (f32[1,1,256,1536]{3,2,1,0:T(8,128)S(1)}, f32[1,1,256,1536]{3,2,1,0:T(8,128)}) fusion(bf16[1,3,256,1536]{3,2,1,0:T(8,128)(2,1)} %reduce-scatter.3.cloned.1.call-done), kind=kLoop, calls=%fused_computation.86 | loop fusion | bytes 6291456 | tf_op jit(solution)/shard_map/slice | solution.py:67
  46.7 0.5 copy.26
  47.2 0.5 copy.27
  47.8 1.9 copy.30
  49.7 1.6 copy.31
  51.5 0.5 copy-done.14
  51.9 0.5 multiply_multiply_fusion.1
  52.4 0.9 copy-done.1
  53.4 0.5 multiply_multiply_fusion
  53.8 0.4 copy-done.6
  54.3 2.3 add_convert_fusion.6
  56.6 3.3 %add_convert_fusion.1 = (bf16[256,12,28]{2,0,1:T(8,128)(2,1)}, bf16[256,12,28]{2,0,1:T(8,128)(2,1)}, bf16[256,12,28]{2,0,1:T(8,128)(2,1)}, bf16[256,12,28]{2,0,1:T(8,128)(2,1)}) fusion(f32[256,12,128]{2,0,1:T(8,128)S(1)} %multiply_multiply_fusion, f32[256,28]{1,0:T(8,128)S(1)} %get-tuple-element.34, f32[256,28]{1,0:T(8,128)S(1)} %get-tuple-element.33, ...), kind=kLoop, calls=%fused_computation.23 | loop fusion | flops 1376256 | bytes 2179072 | tf_op jit(solution)/shard_map/convert.7
  59.9 5.5 %concatenate.12 = bf16[256,12,128]{2,0,1:T(8,128)(2,1)} concatenate(bf16[256,12,8]{2,0,1:T(8,128)(2,1)S(1)} %get-tuple-element.25, bf16[256,12,8]{2,0,1:T(8,128)(2,1)S(1)} %get-tuple-element.26, bf16[256,12,28]{2,0,1:T(8,128)(2,1)} %get-tuple-element.23, bf16[256,12,28]{2,0,1:T(8,128)(2,1)} %get-tuple-element.24, bf16[256,12,28]{2,0,1:T(8,128)(2,1)} %get-tuple-element.16, ...), dimensions={2} | concatenate | bytes 1572864 | tf_op jit(solution)/shard_map/concatenate | solution.py:38
  65.4 1.4 copy.32
  67.1 1.2 slice_bitcast_fusion
  68.3 1.3 pad_maximum_fusion
  69.7 0.7 all-gather.6.cloned.1.call-update
  71.2 15.0 %all-gather = bf16[1,1,64,1536]{3,2,1,0:T(8,128)(2,1)S(1)} all-gather(bf16[1,1,16,1536]{3,2,1,0:T(8,128)(2,1)S(1)} %slice-done), channel_id=2, replica_groups=mesh['groups'=2,'seq'=4,'tensor'=2,'cfg'=2] {'seq'}, dimensions={2}, use_global_device_ids=true | all-gather | bytes 245760 | tf_op jit(solution)/shard_map/all_gather | solution.py:103
  86.2 0.9 reshape.268
  87.3 21.0 %all_gather.13 = bf16[64,1536]{1,0:T(8,128)(2,1)} all-gather(bf16[16,1536]{1,0:T(8,128)(2,1)S(1)} %fusion.28), channel_id=1, replica_groups=mesh['groups'=2,'seq'=4,'tensor'=2,'cfg'=2] {'seq'}, dimensions={0}, use_global_device_ids=true | all-gather | bytes 245760 | tf_op jit(solution)/shard_map/all_gather | solution.py:102
  108.4 4.4 %add_convert_fusion.4 = (bf16[256,12,28]{2,0,1:T(8,128)(2,1)}, bf16[256,12,28]{2,0,1:T(8,128)(2,1)}, bf16[256,12,28]{2,0,1:T(8,128)(2,1)}, bf16[256,12,28]{2,0,1:T(8,128)(2,1)}) fusion(f32[256,12,128]{2,0,1:T(8,128)S(1)} %multiply_multiply_fusion.1, f32[256,28]{1,0:T(8,128)S(1)} %get-tuple-element.34, f32[256,28]{1,0:T(8,128)S(1)} %get-tuple-element.33, ...), kind=kLoop, calls=%fused_computation.31 | loop fusion | flops 1376256 | bytes 2179072 | tf_op jit(solution)/shard_map/convert.13
  112.8 4.6 %concatenate.11 = bf16[256,12,128]{2,0,1:T(8,128)(2,1)S(1)} concatenate(bf16[256,12,8]{2,0,1:T(8,128)(2,1)S(1)} %copy-done.4, bf16[256,12,8]{2,0,1:T(8,128)(2,1)S(1)} %copy-done.3, bf16[256,12,28]{2,0,1:T(8,128)(2,1)} %get-tuple-element.21, bf16[256,12,28]{2,0,1:T(8,128)(2,1)} %get-tuple-element.22, bf16[256,12,28]{2,0,1:T(8,128)(2,1)} %get-tuple-element.10, ...), dimensions={2} | concatenate | bytes 1572864 | tf_op jit(solution)/shard_map/concatenate | solution.py:38
  117.3 1.2 fusion.33
  118.5 71.4 %all-gather.4.cloned.1.call-done = bf16[1024,3072]{1,0:T(8,128)(2,1)} async-done(((bf16[256,3072]{1,0:T(8,128)(2,1)}), bf16[1024,3072]{1,0:T(8,128)(2,1)}) %all-gather.4.cloned.1.call-update) | async-done | bytes 6291472 | tf_op jit(solution)/shard_map/all_gather | solution.py:44
  189.9 4.9 %fusion.30 = (bf16[1024,1536]{1,0:T(8,128)(2,1)S(1)}, bf16[1024,1536]{1,0:T(8,128)(2,1)}) fusion(bf16[1024,3072]{1,0:T(8,128)(2,1)} %all-gather.4.cloned.1.call-done), kind=kLoop, calls=%fused_computation.85 | loop fusion | bytes 12582912 | tf_op jit(solution)/shard_map/split | solution.py:47
  194.8 4.9 %copy.36 = bf16[1024,1536]{0,1:T(8,128)(2,1)} copy(bf16[1024,1536]{1,0:T(8,128)(2,1)} %get-tuple-element.6) | data formatting | bytes 6291456 | tf_op jit(solution)/shard_map/split | solution.py:47
  199.8 2.9 %copy.34 = bf16[1024,1536]{0,1:T(8,128)(2,1)} copy(bf16[1024,1536]{1,0:T(8,128)(2,1)S(1)} %get-tuple-element.5) | data formatting | bytes 6291456 | tf_op jit(solution)/shard_map/split | solution.py:47
  202.7 4.3 %fusion.2 = (f32[12,256]{1,0:T(8,128)S(1)}, f32[12,256,1024]{2,1,0:T(8,128)S(1)}) fusion(bf16[256,12,128]{2,0,1:T(8,128)(2,1)} %copy-done.2, bf16[1024,12,128]{0,2,1:T(8,128)(2,1)} %bitcast.79), kind=kOutput, calls=%fused_computation.3 | convolution fusion | flops 811594752 | bytes 16527360 | tf_op jit(solution)/shard_map/thd,nhd->htn/dot_general | solution.py:86
  207.0 5.3 %fusion.4 = f32[12,256,128]{1,2,0:T(8,128)} fusion(bf16[1024,12,128]{0,2,1:T(8,128)(2,1)} %bitcast.80, f32[12,256,1024]{2,1,0:T(8,128)S(1)} %get-tuple-element.44), kind=kOutput, calls=%fused_computation.5 | convolution fusion | flops 811597824 | bytes 17301504 | tf_op jit(solution)/shard_map/htn,nhd->htd/dot_general | solution.py:91
  212.3 2.0 fusion.17
  214.3 7.5 %convolution_convert_fusion = bf16[256,3072]{1,0:T(8,128)(2,1)} fusion(bf16[256,1536]{0,1:T(8,128)(2,1)S(1)} %bitcast.82, bf16[1536,3072]{1,0:T(8,128)(2,1)} %all-gather.6.cloned.1.call-done), kind=kOutput, calls=%fused_computation.10 | convolution fusion | flops 2416705536 | bytes 11796480 | tf_op jit(solution)/shard_map/dot_general | solution.py:118
  221.8 0.7 copy-done.11
  222.5 25.0 %reduce-scatter.5.cloned.1.call-done = bf16[128,3072]{1,0:T(8,128)(2,1)} async-done(((bf16[256,3072]{1,0:T(8,128)(2,1)}), bf16[128,3072]{1,0:T(8,128)(2,1)}) %reduce-scatter.5.cloned.1.call-update) | async-done | bytes 786448 | tf_op jit(solution)/shard_map/reduce_scatter | solution.py:117
  247.5 1.3 multiply_convert_fusion
  249.5 1.1 collective-permute-done
  250.6 0.9 fusion.21
  (61 shorter events, 1.4 us)
Async XLA Ops:
  6.5 3.2 %copy-start = (bf16[256,3072]{1,0:T(8,128)(2,1)S(1)}, bf16[256,3072]{1,0:T(8,128)(2,1)}, u32[]{:S(2)}) copy-start(bf16[256,3072]{1,0:T(8,128)(2,1)} %param.9) | copy-start | bytes 4718596
  6.5 37.2 %reduce-scatter.3.cloned.1.call-start = ((), (), s32[]{:S(2)}) async-start(), calls=%async_computation.2 | async-start | bytes 7077888 | tf_op jit(solution)/shard_map/reduce_scatter | solution.py:63
  28.3 0.7 copy-start.13
  28.3 2.4 copy-start.15
  28.3 161.6 %all-gather.4.cloned.1.call-start = ((), (), s32[]{:S(2)}) async-start(), calls=%async_computation.3 | async-start | bytes 7864320 | tf_op jit(solution)/shard_map/all_gather | solution.py:44
  51.3 0.6 copy-start.14
  51.9 1.4 copy-start.1
  51.9 1.4 copy-start.12
  53.3 0.9 copy-start.6
  53.4 1.0 copy-start.7
  54.3 2.3 copy-start.5
  69.6 1.5 copy-start.9
  69.6 1.5 slice-start
  69.7 144.6 %all-gather.6.cloned.1.call-start = ((), (), s32[]{:S(2)}) async-start(), calls=%async_computation.4 | async-start | bytes 14155776 | tf_op jit(solution)/shard_map/all_gather | solution.py:116
  70.4 177.1 %reduce-scatter.5.cloned.1.call-start = ((), (), s32[]{:S(2)}) async-start(), calls=%async_computation.5 | async-start | bytes 2359296 | tf_op jit(solution)/shard_map/reduce_scatter | solution.py:117
  108.3 4.4 %copy-start.3 = (bf16[256,12,8]{2,0,1:T(8,128)(2,1)S(1)}, bf16[256,12,8]{2,0,1:T(8,128)(2,1)}, u32[]{:S(2)}) copy-start(bf16[256,12,8]{2,0,1:T(8,128)(2,1)} %get-tuple-element.13) | copy-start | bytes 147460
  108.3 4.4 %copy-start.4 = (bf16[256,12,8]{2,0,1:T(8,128)(2,1)S(1)}, bf16[256,12,8]{2,0,1:T(8,128)(2,1)}, u32[]{:S(2)}) copy-start(bf16[256,12,8]{2,0,1:T(8,128)(2,1)} %get-tuple-element.14) | copy-start | bytes 147460
  112.8 4.6 %copy-start.10 = (bf16[64,1536]{1,0:T(8,128)(2,1)S(1)}, bf16[64,1536]{1,0:T(8,128)(2,1)}, u32[]{:S(2)}) copy-start(bf16[64,1536]{1,0:T(8,128)(2,1)} %all_gather.13) | copy-start | bytes 589828
  117.3 1.2 copy-start.2
  207.0 5.3 %copy-start.8 = (bf16[64,12,128]{2,1,0:T(8,128)(2,1)S(1)}, bf16[64,12,128]{2,1,0:T(8,128)(2,1)}, u32[]{:S(2)}) copy-start(bf16[64,12,128]{2,1,0:T(8,128)(2,1)} %reshape.268) | copy-start | bytes 589828
  221.7 0.7 copy-start.11
  248.8 1.8 collective-permute-start
Sparse Core Ops, SparseCore 0:
  28.4 15.2 reduce-scatter.2
  69.8 120.1 all-gather.3
  191.5 19.9 all-gather.5
  221.9 25.5 reduce-scatter.4
